TPU v7x, 32 devices: a whole 2x2x4 slice. The times are simulated.
32 devices in a mesh: group: 2 (over x), lat: 16 (over z, y, core).
Axes of the slice: x: 2, y: 2, z: 4, core: 2. Of those that a mesh axis runs over, the one named last changes fastest.
Arguments:
- grid_values: bfloat16 [224, 1440, 256], P(('group', 'lat')), parts along dimension 0, may hold values from -630 to 630
- lat_counts: int32 [16], replicated, may hold values from 1 to 7, 96 in all
- owner_wavenumber: int32 [384], replicated, may hold values from 0 to 383, each once
- legendre: bfloat16 [384, 96, 384], P('lat'), may hold values from -0.625 to 0.625
- quad_weight: float32 [96], replicated, may hold values from 0.3 to 3
- spectral_gain: float32 [384, 256], replicated, may hold values from 0.3 to 3
- channel_mix: bfloat16 [256, 256], replicated, may hold values from -0.375 to 0.375
Outputs:
- grid_output: bfloat16 [224, 1440, 256], P(('group', 'lat')), parts along dimension 0
There are 2 independent parts, one for each index of `group`. A program takes and returns all parts, laid end to end along the dimension named above; an argument that names none is the same for every part. Nothing has to cross between parts.
Inputs may be any that keep to these rules, and one draw needn't show every extreme that they name: `lat_counts`: some device has all 7 slots live. `owner_wavenumber`: each wavenumber appears once; device i of lat owns wavenumber slots i * 24 to (i + 1) * 24 - 1.
All inputs are finite; a program needn't handle non-finite values.
Results may differ from a plain program's by a relative error of at most 0.0095.
Values may be sent and summed in bfloat16 or wider, within the bound.
A program may use at most 64 MiB of HBM per device.

v0:
```python
import functools
import math

import jax
import jax.numpy as jnp
import numpy as np
from jax import lax
from jax.experimental import pallas as pl
from jax.experimental.pallas import tpu as pltpu
from jax.sharding import PartitionSpec as P

BLOCK = 8
F32 = jnp.float32
BF16 = jnp.bfloat16


def trig_table(waves, longitudes):
    phase = np.arange(waves)[:, None] * np.arange(longitudes)[None, :] % longitudes
    angle = phase * (2.0 * math.pi / longitudes)
    factor = 1.0 / math.sqrt(longitudes)
    table = np.concatenate([np.cos(angle) * factor, -np.sin(angle) * factor], axis=0)
    return table.astype(BF16)


def greet_all(axis, count, me):
    barrier = pltpu.get_barrier_semaphore()

    def signal(i, carry):
        other = lax.rem(me + i, count)
        pl.semaphore_signal(
            barrier, inc=1, device_id={axis: other}, device_id_type=pl.DeviceIdType.MESH
        )
        return carry

    lax.fori_loop(1, count, signal, 0)
    return barrier


def spectral_kernel(
    axis, n, points, share, counts, owner, x, base_far, waves_lane, legendre_far, quad, gain_far,
    mix, last, back_table, partial,
    sums, full, table, front, normed, spec, recv, gathered, pick, quad_slot, outgoing, result,
    early, base, legendre, gain,
    load, fetch, mom_send, mom_recv, send, arrive, own, back_send, back_arrive, back_own, store,
):
    me = lax.axis_index(axis)
    slots, channels = x.shape[0], x.shape[2]
    everything = n * slots
    live_total, degrees = legendre.shape[1], legendre.shape[2]
    halves = channels // 128
    blocks = spec.shape[0]
    lines = n * 2 * BLOCK
    padded = blocks * BLOCK

    def load_slot(s):
        return pltpu.make_async_copy(x.at[s], normed.at[s], load.at[s])

    def start_load(s, carry):
        load_slot(s).start()
        return carry

    lax.fori_loop(0, slots, start_load, 0)
    base_copy = pltpu.make_async_copy(base_far, base, fetch.at[0])
    legendre_copy = pltpu.make_async_copy(legendre_far, legendre, fetch.at[1])
    gain_copy = pltpu.make_async_copy(gain_far, gain, fetch.at[2])
    base_copy.start()
    legendre_copy.start()
    gain_copy.start()
    barrier = greet_all(axis, n, me)
    live = counts[me]
    group = math.gcd(x.shape[1], 32)
    zero = jnp.zeros((group, channels), F32)

    def add_slot(s, carry):
        first, second = carry
        load_slot(s).wait()
        wide = normed[s].astype(F32).reshape(-1, group, channels)
        weight = jnp.where(s < live, 1.0, 0.0).astype(F32)
        first = first + weight * jnp.sum(wide, axis=0)
        second = second + weight * jnp.sum(wide * wide, axis=0)
        return first, second

    first, second = lax.fori_loop(0, slots, add_slot, (zero, zero))
    sums[me, 0:1, :] = jnp.sum(first, axis=0, keepdims=True)
    sums[me, 1:2, :] = jnp.sum(second, axis=0, keepdims=True)
    pl.semaphore_wait(barrier, n - 1)

    def moment_copy(i):
        other = lax.rem(me + i, n)
        return pltpu.make_async_remote_copy(
            src_ref=sums.at[me], dst_ref=sums.at[me],
            send_sem=mom_send.at[i], recv_sem=mom_recv.at[i],
            device_id={axis: other}, device_id_type=pl.DeviceIdType.MESH,
        )

    def start_moment(i, carry):
        moment_copy(i).start()
        return carry

    def wait_moment(i, carry):
        moment_copy(i).wait()
        return carry

    lax.fori_loop(1, n, start_moment, 0)
    waves = base.shape[0] // 2
    natural = lax.broadcasted_iota(jnp.int32, (waves, n * padded), 0)
    chosen = jnp.where(natural == waves_lane[...], 1.0, 0.0).astype(BF16)
    base_copy.wait()
    for t in range(2):
        full[t] = lax.dot_general(
            chosen, base[t * waves : (t + 1) * waves], (((0,), (0,)), ((), ())),
            preferred_element_type=F32,
        )

    def order_rows(o, carry):
        for b in range(blocks):
            begin = pl.multiple_of(o * padded + b * BLOCK, BLOCK)
            both = [full[t, pl.ds(begin, BLOCK), :] for t in range(2)]
            begin = pl.multiple_of((b * n + o) * 2 * BLOCK, 2 * BLOCK)
            table[pl.ds(begin, 2 * BLOCK), :] = jnp.concatenate(both, axis=0).astype(BF16)
        return carry

    lax.fori_loop(0, n, order_rows, 0)
    lax.fori_loop(1, n, wait_moment, 0)
    both = jnp.sum(sums[...], axis=0)
    mean = both[0:1] / points
    variance = both[1:2] / points - mean * mean
    scale = lax.rsqrt(variance + 1e-05)

    def block_copy(b, i):
        other = lax.rem(me + i, n)
        return pltpu.make_async_remote_copy(
            src_ref=spec.at[b, other], dst_ref=recv.at[b, me],
            send_sem=send.at[b, i], recv_sem=arrive.at[b, i],
            device_id={axis: other}, device_id_type=pl.DeviceIdType.MESH,
        )

    for b in range(blocks):

        def slot_step(s, carry):
            if b == 0:
                weight = jnp.where(s < live, 1.0, 0.0).astype(F32)
                normed[s] = ((normed[s].astype(F32) - mean) * scale * weight).astype(BF16)
            out = jnp.dot(
                table[b * lines : (b + 1) * lines], normed[s], preferred_element_type=F32
            )
            spec[b, :, s] = out.astype(BF16).reshape(n, 2 * BLOCK, channels)
            if b == 0:

                def start_slot(i, inner):
                    other = lax.rem(me + i, n)
                    pltpu.make_async_remote_copy(
                        src_ref=spec.at[b, other, s], dst_ref=recv.at[b, me, s],
                        send_sem=send.at[b, i], recv_sem=arrive.at[b, i],
                        device_id={axis: other}, device_id_type=pl.DeviceIdType.MESH,
                    ).start()
                    return inner

                lax.fori_loop(1, n, start_slot, 0)
            return carry

        lax.fori_loop(0, slots, slot_step, 0)
        if b > 0:

            def start_block(i, carry):
                block_copy(b, i).start()
                return carry

            lax.fori_loop(1, n, start_block, 0)
        pltpu.make_async_copy(spec.at[b, me], recv.at[b, me], own.at[b]).start()

    late = (blocks - 1) * lines
    back_table[...] = table[late:].T
    if blocks > 1:
        front[...] = table[:late].T
    legendre_copy.wait()
    gain_copy.wait()
    row = lax.broadcasted_iota(jnp.int32, (everything, live_total), 0)
    lane = lax.broadcasted_iota(jnp.int32, (everything, live_total), 1)
    pick[...] = jnp.zeros_like(pick)

    def mark(i, begin):
        within = row - i * slots
        hit = (within >= 0) & (within < counts[i]) & (lane == begin + within)
        pick[...] += jnp.where(hit, 1.0, 0.0).astype(F32)
        return begin + counts[i]

    lax.fori_loop(0, n, mark, jnp.int32(0))
    quad_slot[...] = jnp.broadcast_to(
        jnp.sum(pick[...] * quad[...], axis=1, keepdims=True), quad_slot.shape
    )
    degree = lax.broadcasted_iota(jnp.int32, (degrees, channels), 0)

    def landing(b):
        return early.at[b, me] if b < blocks - 1 else last.at[me]

    def return_copy(b, i):
        other = lax.rem(me + i, n)
        return pltpu.make_async_remote_copy(
            src_ref=outgoing.at[b, other], dst_ref=landing(b),
            send_sem=back_send.at[b, i], recv_sem=back_arrive.at[b, i],
            device_id={axis: other}, device_id_type=pl.DeviceIdType.MESH,
        )

    for b in range(blocks):
        count = min(BLOCK, share - b * BLOCK)
        if count < BLOCK:
            result[...] = jnp.zeros_like(result)

        def wait_block(i, carry):
            block_copy(b, i).wait()
            return carry

        lax.fori_loop(1, n, wait_block, 0)
        pltpu.make_async_copy(spec.at[b, me], recv.at[b, me], own.at[b]).wait()

        def widen(i, carry):
            for s in range(slots):
                wide = recv[b, i, s].astype(F32)
                begin = pl.multiple_of((i * slots + s) * 2 * BLOCK, 8)
                for h in range(halves):
                    gathered[h, pl.ds(begin, 2 * BLOCK), :] = wide[:, h * 128 : (h + 1) * 128]
            return carry

        lax.fori_loop(0, n, widen, 0)

        def wave_step(r, carry):
            wave = owner[me * share + b * BLOCK + r]
            expanded = jnp.dot(
                pick[...].astype(BF16), legendre[b * BLOCK + r], preferred_element_type=F32
            ).astype(BF16)
            pieces = []
            for t in range(2):
                for h in range(halves):
                    piece = gathered[h, pl.ds(t * BLOCK + r, everything, stride=2 * BLOCK), :]
                    pieces.append((piece * quad_slot[...]).astype(BF16))
            weighted = jnp.concatenate(pieces, axis=1)
            coefficient = lax.dot_general(
                expanded, weighted, (((0,), (0,)), ((), ())), preferred_element_type=F32
            )
            kept = degree >= wave
            factor = jnp.where(wave > 0, 2.0, 1.0).astype(F32)
            mixed = []
            for t in range(2):
                part = coefficient[:, t * channels : (t + 1) * channels] * gain[...]
                part = jnp.where(kept, part, 0.0).astype(BF16)
                mixed.append(jnp.dot(part, mix[...], preferred_element_type=F32).astype(BF16))
            synthesis = jnp.dot(
                expanded, jnp.concatenate(mixed, axis=1), preferred_element_type=F32
            ) * factor
            for t in range(2):
                for h in range(halves):
                    begin = t * channels + h * 128
                    result[h, pl.ds(t * BLOCK + r, everything, stride=2 * BLOCK), :] = synthesis[
                        :, begin : begin + 128
                    ]
            return carry

        lax.fori_loop(0, count, wave_step, 0)

        def narrow(i, carry):
            for s in range(slots):
                begin = pl.multiple_of((i * slots + s) * 2 * BLOCK, 8)
                outgoing[b, i, s] = jnp.concatenate(
                    [result[h, pl.ds(begin, 2 * BLOCK), :] for h in range(halves)], axis=1
                ).astype(BF16)
            return carry

        lax.fori_loop(0, n, narrow, 0)

        def start_return(i, carry):
            return_copy(b, i).start()
            return carry

        lax.fori_loop(1, n, start_return, 0)
        pltpu.make_async_copy(outgoing.at[b, me], landing(b), back_own.at[b]).start()

    def settle(b):
        def wait_return(i, carry):
            return_copy(b, i).wait()
            return carry

        lax.fori_loop(1, n, wait_return, 0)
        pltpu.make_async_copy(outgoing.at[b, me], landing(b), back_own.at[b]).wait()

    def store_slot(s):
        return pltpu.make_async_copy(normed.at[s], partial.at[s], store.at[s])

    for b in range(blocks - 1):
        settle(b)

    def partial_slot(s, carry):
        if blocks > 1:
            block = early[:, :, s].reshape(late, channels)
            normed[s] = jnp.dot(front[...], block, preferred_element_type=F32).astype(BF16)
        else:
            normed[s] = jnp.zeros(normed.shape[1:], BF16)
        store_slot(s).start()
        return carry

    def wait_store(s, carry):
        store_slot(s).wait()
        return carry

    lax.fori_loop(0, slots, partial_slot, 0)
    lax.fori_loop(0, slots, wait_store, 0)
    settle(blocks - 1)


def inverse_kernel(last, table, partial, out):
    block = last[...].reshape(table.shape[1], last.shape[-1])
    total = jnp.dot(table[...], block, preferred_element_type=F32)
    out[0] = (partial[0].astype(F32) + total).astype(BF16)


def body(
    n, grid_values, lat_counts, owner_wavenumber, legendre, quad_weight, spectral_gain, channel_mix
):
    slots, longitudes, channels = grid_values.shape
    waves = owner_wavenumber.shape[0]
    share, live_total, degrees = legendre.shape
    blocks = -(-share // BLOCK)
    padded = blocks * BLOCK
    everything = n * slots
    base = jnp.asarray(trig_table(waves, longitudes))
    slot_waves = owner_wavenumber.reshape(n, share)
    slot_waves = jnp.pad(slot_waves, ((0, 0), (0, padded - share)), constant_values=-1)
    waves_lane = slot_waves.reshape(1, n * padded)

    vmem = pl.BlockSpec(memory_space=pltpu.VMEM)
    smem = pl.BlockSpec(memory_space=pltpu.SMEM)
    anywhere = pl.BlockSpec(memory_space=pl.ANY)
    limit = 60 * 1024 * 1024
    packet = (blocks, n, slots, 2 * BLOCK, channels)
    copies = pltpu.SemaphoreType.DMA
    lines = n * 2 * BLOCK
    last, back_table, partial = pl.pallas_call(
        functools.partial(spectral_kernel, "lat", n, live_total * longitudes, share),
        out_shape=(
            jax.ShapeDtypeStruct(packet[1:], BF16),
            jax.ShapeDtypeStruct((longitudes, lines), BF16),
            jax.ShapeDtypeStruct((slots, longitudes, channels), BF16),
        ),
        in_specs=[smem, smem, anywhere, anywhere, vmem, anywhere, vmem, anywhere, vmem],
        out_specs=(anywhere, vmem, anywhere),
        scratch_shapes=[
            pltpu.VMEM((n, 2, channels), F32),
            pltpu.VMEM((2, n * padded, longitudes), F32),
            pltpu.VMEM((blocks * lines, longitudes), BF16),
            pltpu.VMEM((longitudes, max(blocks - 1, 1) * lines), BF16),
            pltpu.VMEM((slots, longitudes, channels), BF16),
            pltpu.VMEM(packet, BF16),
            pltpu.VMEM(packet, BF16),
            pltpu.VMEM((channels // 128, everything * 2 * BLOCK, 128), F32),
            pltpu.VMEM((everything, live_total), F32),
            pltpu.VMEM((everything, 128), F32),
            pltpu.VMEM(packet, BF16),
            pltpu.VMEM((channels // 128, everything * 2 * BLOCK, 128), F32),
            pltpu.VMEM((max(blocks - 1, 1),) + packet[1:], BF16),
            pltpu.VMEM(base.shape, BF16),
            pltpu.VMEM(legendre.shape, BF16),
            pltpu.VMEM(spectral_gain.shape, F32),
            copies((slots,)), copies((3,)),
            copies((n,)), copies((n,)),
            copies((blocks, n)), copies((blocks, n)), copies((blocks,)),
            copies((blocks, n)), copies((blocks, n)), copies((blocks,)),
            copies((slots,)),
        ],
        compiler_params=pltpu.CompilerParams(
            collective_id=0, has_side_effects=True, vmem_limit_bytes=limit
        ),
    )(
        lat_counts, owner_wavenumber, grid_values, base, waves_lane, legendre,
        quad_weight.reshape(1, live_total), spectral_gain, channel_mix,
    )

    return pl.pallas_call(
        inverse_kernel,
        grid=(slots,),
        out_shape=jax.ShapeDtypeStruct((slots, longitudes, channels), BF16),
        in_specs=[
            pl.BlockSpec((n, None, 2 * BLOCK, channels), lambda s: (0, s, 0, 0)),
            pl.BlockSpec((longitudes, lines), lambda s: (0, 0)),
            pl.BlockSpec((1, longitudes, channels), lambda s: (s, 0, 0)),
        ],
        out_specs=pl.BlockSpec((1, longitudes, channels), lambda s: (s, 0, 0)),
        compiler_params=pltpu.CompilerParams(vmem_limit_bytes=limit),
    )(last, back_table, partial)


def solution(mesh):
    return jax.shard_map(
        functools.partial(body, mesh.shape["lat"]),
        mesh=mesh,
        in_specs=(P(("group", "lat"), None, None), P(), P(), P("lat", None, None), P(), P(), P()),
        out_specs=P(("group", "lat"), None, None),
        check_vma=False,
    )
```

profile of v0, /device:TPU:13, one launch (start us, length us, event | category | flops | bytes accessed | tf_op | source)
XLA Modules:
  0.0 142.9 jit_solution(18325281875135338358)
XLA Ops:
  0.0 1.2 reshape.8.waves_lane
  1.2 132.7 %shard_map.82 = (bf16[16,7,16,256]{3,2,1,0:T(8,128)(2,1)}, bf16[1440,256]{1,0:T(8,128)(2,1)}, bf16[7,1440,256]{2,1,0:T(8,128)(2,1)}) custom-call(s32[16]{0:T(128)} %counts.1, s32[384]{0:T(512)} %owner.1, bf16[7,1440,256]{2,1,0:T(8,128)(2,1)} %x.1, bf16[768,1440]{1,0:T(8,128)(2,1)} %constant.1.clone.base_far, s32[1,384]{1,0:T(1,128)} %reshape.8.waves_lane, ...), custom_call_target="tpu_custom_call" | custom-call | tf_op jit(solution)/shard_map/pallas_call | solution.py:337
  134.0 8.9 %shard_map.83 = bf16[7,1440,256]{2,1,0:T(8,128)(2,1)} custom-call(bf16[16,7,16,256]{3,2,1,0:T(8,128)(2,1)} %get-tuple-element.8.last, bf16[1440,256]{1,0:T(8,128)(2,1)} %get-tuple-element.9.table, bf16[7,1440,256]{2,1,0:T(8,128)(2,1)} %get-tuple-element.10.partial), custom_call_target="tpu_custom_call" | custom-call | tf_op jit(solution)/shard_map/pallas_call | solution.py:377
where the time goes:
time: 143 us
  Pallas kernels  142 us (99%)
    pallas_call x1, Pallas kernels, body(): pl.pallas_call(functools.partial(spectral_kernel, 'lat', n, live_total *...  133 us
    pallas_call x1, Pallas kernels, body(): pl.pallas_call(inverse_kernel, grid=(slots,), out_shape=jax.ShapeDtypeStr...  8.9 us

commit v1 on v0

v1 whole, which is shorter than its diff:
```python
import functools
import math

import jax
import jax.numpy as jnp
import numpy as np
from jax import lax
from jax.experimental import pallas as pl
from jax.experimental.pallas import tpu as pltpu
from jax.sharding import PartitionSpec as P

BLOCK = 8
F32 = jnp.float32
BF16 = jnp.bfloat16


def trig_table(waves, longitudes):
    phase = np.arange(waves)[:, None] * np.arange(longitudes)[None, :] % longitudes
    angle = phase * (2.0 * math.pi / longitudes)
    factor = 1.0 / math.sqrt(longitudes)
    table = np.concatenate([np.cos(angle) * factor, -np.sin(angle) * factor], axis=0)
    return table.astype(BF16)


def greet_all(axis, count, me):
    barrier = pltpu.get_barrier_semaphore()

    def signal(i, carry):
        other = lax.rem(me + i, count)
        pl.semaphore_signal(
            barrier, inc=1, device_id={axis: other}, device_id_type=pl.DeviceIdType.MESH
        )
        return carry

    lax.fori_loop(1, count, signal, 0)
    return barrier


def spectral_kernel(
    axis, n, points, share, counts, owner, row_sum, x, base_far, legendre_far, quad, gain_far,
    mix, last, back_table, partial,
    sums, rows, hot, table, front, spec, recv, gathered, pick, quad_slot, outgoing, result,
    early, base, legendre, gain,
    load, fetch, mom_send, mom_recv, send, arrive, own, back_send, back_arrive, back_own,
):
    me = lax.axis_index(axis)
    slots, longitudes, channels = x.shape
    everything = n * slots
    live_total, degrees = legendre.shape[1], legendre.shape[2]
    halves = channels // 128
    blocks = spec.shape[0]
    lines = n * 2 * BLOCK
    waves = base.shape[0] // 2

    def load_slot(s):
        return pltpu.make_async_copy(x.at[s], partial.at[s], load.at[s])

    def start_load(s, carry):
        load_slot(s).start()
        return carry

    base_copy = pltpu.make_async_copy(base_far, base, fetch.at[0])
    legendre_copy = pltpu.make_async_copy(legendre_far, legendre, fetch.at[1])
    gain_copy = pltpu.make_async_copy(gain_far, gain, fetch.at[2])
    base_copy.start()
    lax.fori_loop(0, slots, start_load, 0)
    legendre_copy.start()
    gain_copy.start()
    barrier = greet_all(axis, n, me)

    row_of = lax.broadcasted_iota(jnp.int32, (BLOCK, waves), 0)
    lane_of = lax.broadcasted_iota(jnp.int32, (BLOCK, waves), 1)

    def choose_rows(o, carry):
        for b in range(blocks):
            count = min(BLOCK, share - b * BLOCK)
            held = jnp.full((BLOCK, waves), -1, jnp.int32)
            for r in range(count):
                held = jnp.where(row_of == r, owner[o * share + b * BLOCK + r], held)
            begin = pl.multiple_of((b * n + o) * BLOCK, BLOCK)
            hot[pl.ds(begin, BLOCK), :] = jnp.where(lane_of == held, 1.0, 0.0).astype(F32)
        return carry

    lax.fori_loop(0, n, choose_rows, 0)
    live = counts[me]
    group = math.gcd(longitudes, 32)

    def build_table(b):
        chosen = hot[b * n * BLOCK : (b + 1) * n * BLOCK, :].astype(BF16)
        both = [
            jnp.dot(chosen, base[t * waves : (t + 1) * waves], preferred_element_type=F32)
            for t in range(2)
        ]
        both = [part.reshape(n, 1, BLOCK, longitudes) for part in both]
        both = jnp.concatenate(both, axis=1).reshape(lines, longitudes)
        table[b * lines : (b + 1) * lines] = both.astype(BF16)

    def transform(b, s):
        out = jnp.dot(table[b * lines : (b + 1) * lines], partial[s], preferred_element_type=F32)
        spec[b, :, s] = out.astype(BF16).reshape(n, 2 * BLOCK, channels)

    def add_slot(s, second):
        wide = partial[s].astype(F32).reshape(-1, group, channels)
        weight = jnp.where(s < live, 1.0, 0.0).astype(F32)
        first = weight * jnp.sum(wide, axis=0)
        sums[me, pl.ds(s, 1), :] = jnp.sum(first, axis=0, keepdims=True)
        return second + weight * jnp.sum(wide * wide, axis=0)

    def slice_copy(b, i, first, size):
        other = lax.rem(me + i, n)
        return pltpu.make_async_remote_copy(
            src_ref=spec.at[b, other, pl.ds(first, size)],
            dst_ref=recv.at[b, me, pl.ds(first, size)],
            send_sem=send.at[b, i], recv_sem=arrive.at[b, i],
            device_id={axis: other}, device_id_type=pl.DeviceIdType.MESH,
        )

    def block_copy(b, i):
        return slice_copy(b, i, 0, slots)

    def send_slices(b, first, size):
        def start_slices(i, carry):
            slice_copy(b, i, first, size).start()
            return carry

        lax.fori_loop(1, n, start_slices, 0)

    def moment_copy(i):
        other = lax.rem(me + i, n)
        return pltpu.make_async_remote_copy(
            src_ref=sums.at[me], dst_ref=sums.at[me],
            send_sem=mom_send.at[i], recv_sem=mom_recv.at[i],
            device_id={axis: other}, device_id_type=pl.DeviceIdType.MESH,
        )

    def start_moment(i, carry):
        moment_copy(i).start()
        return carry

    def wait_moment(i, carry):
        moment_copy(i).wait()
        return carry

    def own_copy(b):
        return pltpu.make_async_copy(spec.at[b, me], recv.at[b, me], own.at[b])

    base_copy.wait()
    build_table(0)
    load_slot(0).wait()
    transform(0, 0)
    pl.semaphore_wait(barrier, n - 1)
    send_slices(0, 0, 1)

    def first_slot(s, carry):
        load_slot(s).wait()
        transform(0, s)
        return carry

    cuts = [1, 1 + (slots - 1) // 3, slots]
    for first, end in zip(cuts[:-1], cuts[1:]):
        if end > first:
            lax.fori_loop(first, end, first_slot, 0)
            send_slices(0, first, end - first)
    own_copy(0).start()
    second = lax.fori_loop(0, slots, add_slot, jnp.zeros((group, channels), F32))
    sums[me, slots : slots + 1, :] = jnp.sum(second, axis=0, keepdims=True)
    lax.fori_loop(1, n, start_moment, 0)
    for b in range(1, blocks):
        build_table(b)

        def slot_step(s, carry):
            transform(b, s)
            return carry

        lax.fori_loop(0, slots, slot_step, 0)
        send_slices(b, 0, slots)
        own_copy(b).start()

    late = (blocks - 1) * lines
    back_table[...] = table[late:].T
    if blocks > 1:
        front[...] = table[:late].T
    legendre_copy.wait()
    gain_copy.wait()
    row = lax.broadcasted_iota(jnp.int32, (everything, live_total), 0)
    lane = lax.broadcasted_iota(jnp.int32, (everything, live_total), 1)
    pick[...] = jnp.zeros_like(pick)

    def mark(i, begin):
        within = row - i * slots
        hit = (within >= 0) & (within < counts[i]) & (lane == begin + within)
        pick[...] += jnp.where(hit, 1.0, 0.0).astype(F32)
        return begin + counts[i]

    lax.fori_loop(0, n, mark, jnp.int32(0))
    quad_slot[...] = jnp.broadcast_to(
        jnp.sum(pick[...] * quad[...], axis=1, keepdims=True), quad_slot.shape
    )
    degree = lax.broadcasted_iota(jnp.int32, (degrees, channels), 0)
    lax.fori_loop(1, n, wait_moment, 0)
    totals = jnp.sum(sums[...], axis=0)
    mean = jnp.sum(totals[0:slots], axis=0, keepdims=True) / points
    variance = totals[slots : slots + 1] / points - mean * mean
    gain[...] = gain[...] * lax.rsqrt(variance + 1e-05)
    for i in range(n):
        rows[i * slots : (i + 1) * slots, :] = sums[i, 0:slots, :]
    level = float(np.asarray(1.0 / math.sqrt(longitudes)).astype(BF16))

    def landing(b):
        return early.at[b, me] if b < blocks - 1 else last.at[me]

    def return_copy(b, i):
        other = lax.rem(me + i, n)
        return pltpu.make_async_remote_copy(
            src_ref=outgoing.at[b, other], dst_ref=landing(b),
            send_sem=back_send.at[b, i], recv_sem=back_arrive.at[b, i],
            device_id={axis: other}, device_id_type=pl.DeviceIdType.MESH,
        )

    for b in range(blocks):
        count = min(BLOCK, share - b * BLOCK)
        if count < BLOCK:
            result[...] = jnp.zeros_like(result)

        def wait_block(i, carry):
            block_copy(b, i).wait()
            return carry

        lax.fori_loop(1, n, wait_block, 0)
        own_copy(b).wait()

        def widen(i, carry):
            for s in range(slots):
                wide = recv[b, i, s].astype(F32)
                begin = pl.multiple_of((i * slots + s) * 2 * BLOCK, 8)
                for h in range(halves):
                    gathered[h, pl.ds(begin, 2 * BLOCK), :] = wide[:, h * 128 : (h + 1) * 128]
            return carry

        lax.fori_loop(0, n, widen, 0)

        def wave_step(r, carry):
            wave = owner[me * share + b * BLOCK + r]
            expanded = jnp.dot(
                pick[...].astype(BF16), legendre[b * BLOCK + r], preferred_element_type=F32
            ).astype(BF16)
            pieces = []
            for t in range(2):
                for h in range(halves):
                    lanes = slice(h * 128, (h + 1) * 128)
                    piece = gathered[h, pl.ds(t * BLOCK + r, everything, stride=2 * BLOCK), :]
                    if t == 0:
                        piece = jnp.where(wave == 0, rows[:, lanes] * level, piece)
                    piece = piece - mean[:, lanes] * row_sum[t * waves + wave]
                    pieces.append((piece * quad_slot[...]).astype(BF16))
            weighted = jnp.concatenate(pieces, axis=1)
            coefficient = lax.dot_general(
                expanded, weighted, (((0,), (0,)), ((), ())), preferred_element_type=F32
            )
            kept = degree >= wave
            factor = jnp.where(wave > 0, 2.0, 1.0).astype(F32)
            mixed = []
            for t in range(2):
                part = coefficient[:, t * channels : (t + 1) * channels] * gain[...]
                part = jnp.where(kept, part, 0.0).astype(BF16)
                mixed.append(jnp.dot(part, mix[...], preferred_element_type=F32).astype(BF16))
            synthesis = jnp.dot(
                expanded, jnp.concatenate(mixed, axis=1), preferred_element_type=F32
            ) * factor
            for t in range(2):
                for h in range(halves):
                    begin = t * channels + h * 128
                    result[h, pl.ds(t * BLOCK + r, everything, stride=2 * BLOCK), :] = synthesis[
                        :, begin : begin + 128
                    ]
            return carry

        lax.fori_loop(0, count, wave_step, 0)

        def narrow(i, carry):
            for s in range(slots):
                begin = pl.multiple_of((i * slots + s) * 2 * BLOCK, 8)
                outgoing[b, i, s] = jnp.concatenate(
                    [result[h, pl.ds(begin, 2 * BLOCK), :] for h in range(halves)], axis=1
                ).astype(BF16)
            return carry

        lax.fori_loop(0, n, narrow, 0)

        def start_return(i, carry):
            return_copy(b, i).start()
            return carry

        lax.fori_loop(1, n, start_return, 0)
        pltpu.make_async_copy(outgoing.at[b, me], landing(b), back_own.at[b]).start()

    def settle(b):
        def wait_return(i, carry):
            return_copy(b, i).wait()
            return carry

        lax.fori_loop(1, n, wait_return, 0)
        pltpu.make_async_copy(outgoing.at[b, me], landing(b), back_own.at[b]).wait()

    for b in range(blocks - 1):
        settle(b)

    def partial_slot(s, carry):
        if blocks > 1:
            block = early[:, :, s].reshape(late, channels)
            partial[s] = jnp.dot(front[...], block, preferred_element_type=F32).astype(BF16)
        else:
            partial[s] = jnp.zeros(partial.shape[1:], BF16)
        return carry

    lax.fori_loop(0, slots, partial_slot, 0)
    settle(blocks - 1)


def inverse_kernel(last, table, partial, out, held, store):
    slots = partial.shape[0]

    def store_slot(s):
        return pltpu.make_async_copy(held.at[s], out.at[s], store.at[s])

    def finish_slot(s, carry):
        block = last[:, s].reshape(table.shape[1], last.shape[-1])
        total = jnp.dot(table[...], block, preferred_element_type=F32)
        held[s] = (partial[s].astype(F32) + total).astype(BF16)
        store_slot(s).start()
        return carry

    def wait_store(s, carry):
        store_slot(s).wait()
        return carry

    lax.fori_loop(0, slots, finish_slot, 0)
    lax.fori_loop(0, slots, wait_store, 0)


def body(
    n, grid_values, lat_counts, owner_wavenumber, legendre, quad_weight, spectral_gain, channel_mix
):
    slots, longitudes, channels = grid_values.shape
    waves = owner_wavenumber.shape[0]
    share, live_total, degrees = legendre.shape
    blocks = -(-share // BLOCK)
    padded = blocks * BLOCK
    everything = n * slots
    trig = trig_table(waves, longitudes)
    base = jnp.asarray(trig)
    row_sum = jnp.asarray(trig.astype(np.float64).sum(axis=1).astype(np.float32))

    vmem = pl.BlockSpec(memory_space=pltpu.VMEM)
    smem = pl.BlockSpec(memory_space=pltpu.SMEM)
    anywhere = pl.BlockSpec(memory_space=pl.ANY)
    limit = 48 * 1024 * 1024
    packet = (blocks, n, slots, 2 * BLOCK, channels)
    copies = pltpu.SemaphoreType.DMA
    lines = n * 2 * BLOCK
    last, back_table, partial = pl.pallas_call(
        functools.partial(spectral_kernel, "lat", n, live_total * longitudes, share),
        out_shape=(
            pltpu.VMEM(packet[1:], BF16),
            pltpu.VMEM((longitudes, lines), BF16),
            pltpu.VMEM((slots, longitudes, channels), BF16),
        ),
        in_specs=[smem, smem, smem, anywhere, anywhere, anywhere, vmem, anywhere, vmem],
        out_specs=(vmem, vmem, vmem),
        scratch_shapes=[
            pltpu.VMEM((n, slots + 1, channels), F32),
            pltpu.VMEM((everything, channels), F32),
            pltpu.VMEM((n * padded, waves), F32),
            pltpu.VMEM((blocks * lines, longitudes), BF16),
            pltpu.VMEM((longitudes, max(blocks - 1, 1) * lines), BF16),
            pltpu.VMEM(packet, BF16),
            pltpu.VMEM(packet, BF16),
            pltpu.VMEM((channels // 128, everything * 2 * BLOCK, 128), F32),
            pltpu.VMEM((everything, live_total), F32),
            pltpu.VMEM((everything, 128), F32),
            pltpu.VMEM(packet, BF16),
            pltpu.VMEM((channels // 128, everything * 2 * BLOCK, 128), F32),
            pltpu.VMEM((max(blocks - 1, 1),) + packet[1:], BF16),
            pltpu.VMEM(base.shape, BF16),
            pltpu.VMEM(legendre.shape, BF16),
            pltpu.VMEM(spectral_gain.shape, F32),
            copies((slots,)), copies((3,)),
            copies((n,)), copies((n,)),
            copies((blocks, n)), copies((blocks, n)), copies((blocks,)),
            copies((blocks, n)), copies((blocks, n)), copies((blocks,)),
        ],
        compiler_params=pltpu.CompilerParams(
            collective_id=0, has_side_effects=True, vmem_limit_bytes=limit
        ),
    )(
        lat_counts, owner_wavenumber, row_sum, grid_values, base, legendre,
        quad_weight.reshape(1, live_total), spectral_gain, channel_mix,
    )

    return pl.pallas_call(
        inverse_kernel,
        out_shape=jax.ShapeDtypeStruct((slots, longitudes, channels), BF16),
        in_specs=[vmem, vmem, vmem],
        out_specs=anywhere,
        scratch_shapes=[
            pltpu.VMEM((slots, longitudes, channels), BF16),
            copies((slots,)),
        ],
        compiler_params=pltpu.CompilerParams(vmem_limit_bytes=16 * 1024 * 1024),
    )(*[pltpu.with_memory_space_constraint(v, pltpu.VMEM) for v in (last, back_table, partial)])


def solution(mesh):
    return jax.shard_map(
        functools.partial(body, mesh.shape["lat"]),
        mesh=mesh,
        in_specs=(P(("group", "lat"), None, None), P(), P(), P("lat", None, None), P(), P(), P()),
        out_specs=P(("group", "lat"), None, None),
        check_vma=False,
    )
```

time: 143 us -> 133 us (0.930)
  Pallas kernels: 142 us -> 133 us
    pallas_call x1, Pallas kernels: 8.9 us -> 3.42 us  [body(): pl.pallas_call(inverse_kernel, out_shape=jax.ShapeDtypeStruct((slots, lon...]
    pallas_call x1, Pallas kernels: 133 us -> 130 us  [body(): pl.pallas_call(functools.partial(spectral_kernel, 'lat', n, live_total *...]
where the time goes in v1:
time: 133 us
  Pallas kernels  133 us (100%)
    pallas_call x1, Pallas kernels, body(): pl.pallas_call(functools.partial(spectral_kernel, 'lat', n, live_total *...  130 us
    pallas_call x1, Pallas kernels, body(): pl.pallas_call(inverse_kernel, out_shape=jax.ShapeDtypeStruct((slots, lon...  3.42 us

profile of v1, /device:TPU:13, one launch (start us, length us, event | category | flops | bytes accessed | tf_op | source)
XLA Modules:
  0.0 133.1 jit_solution(6137607114128148886)
XLA Ops:
  0.0 129.7 %shard_map.91 = (bf16[16,7,16,256]{3,2,1,0:T(8,128)(2,1)S(1)}, bf16[1440,256]{1,0:T(8,128)(2,1)S(1)}, bf16[7,1440,256]{2,1,0:T(8,128)(2,1)S(1)}) custom-call(s32[16]{0:T(128)} %counts.1, s32[384]{0:T(512)} %owner.1, f32[768]{0:T(1024)} %constant.5.clone.row_sum, bf16[7,1440,256]{2,1,0:T(8,128)(2,1)} %x.1, bf16[768,1440]{1,0:T(8,128)(2,1)} %constant.4.clone.base_far, ...), custom_call_target="tpu_custom_call" | custom-call | tf_op jit(solution)/shard_map/pallas_call | solution.py:361
  129.7 3.4 %shard_map.92 = bf16[7,1440,256]{2,1,0:T(8,128)(2,1)} custom-call(bf16[16,7,16,256]{3,2,1,0:T(8,128)(2,1)S(1)} %get-tuple-element.8.last, bf16[1440,256]{1,0:T(8,128)(2,1)S(1)} %get-tuple-element.9.table, bf16[7,1440,256]{2,1,0:T(8,128)(2,1)S(1)} %get-tuple-element.10.partial), custom_call_target="tpu_custom_call" | custom-call | tf_op jit(solution)/shard_map/pallas_call | solution.py:400

commit v2 on v1

--- a/solution.py
+++ b/solution.py
@@ -10,6 +10,7 @@
 from jax.sharding import PartitionSpec as P
 
 BLOCK = 8
+TAIL = 1
 F32 = jnp.float32
 BF16 = jnp.bfloat16
 
@@ -39,8 +40,8 @@
 def spectral_kernel(
     axis, n, points, share, counts, owner, row_sum, x, base_far, legendre_far, quad, gain_far,
     mix, last, back_table, partial,
-    sums, rows, hot, table, front, spec, recv, gathered, pick, quad_slot, outgoing, result,
-    early, base, legendre, gain,
+    sums, zero, hot, table, front, spec, recv, gathered, pick, quad_slot, outgoing, result,
+    early, late, base, legendre, gain,
     load, fetch, mom_send, mom_recv, send, arrive, own, back_send, back_arrive, back_own,
 ):
     me = lax.axis_index(axis)
@@ -51,6 +52,7 @@
     blocks = spec.shape[0]
     lines = n * 2 * BLOCK
     waves = base.shape[0] // 2
+    ready = slots - last.shape[1]
 
     def load_slot(s):
         return pltpu.make_async_copy(x.at[s], partial.at[s], load.at[s])
@@ -82,6 +84,7 @@
         return carry
 
     lax.fori_loop(0, n, choose_rows, 0)
+    zero[...] = jnp.broadcast_to(hot[:, 0:1], zero.shape)
     live = counts[me]
     group = math.gcd(longitudes, 32)
 
@@ -97,14 +100,20 @@
 
     def transform(b, s):
         out = jnp.dot(table[b * lines : (b + 1) * lines], partial[s], preferred_element_type=F32)
-        spec[b, :, s] = out.astype(BF16).reshape(n, 2 * BLOCK, channels)
-
-    def add_slot(s, second):
+        out = out.reshape(n, 2, BLOCK, channels)
+        real, imag = out[:, 0], out[:, 1]
+        flag = zero[b * n * BLOCK : (b + 1) * n * BLOCK].reshape(n, BLOCK, channels)
+        imag = imag + flag * (real - real.astype(BF16).astype(F32))
+        out = jnp.concatenate([real, imag], axis=1)
+        spec[b, :, s] = out.astype(BF16)
+
+    def add_slot(s, carry):
+        first, second = carry
         wide = partial[s].astype(F32).reshape(-1, group, channels)
         weight = jnp.where(s < live, 1.0, 0.0).astype(F32)
-        first = weight * jnp.sum(wide, axis=0)
-        sums[me, pl.ds(s, 1), :] = jnp.sum(first, axis=0, keepdims=True)
-        return second + weight * jnp.sum(wide * wide, axis=0)
+        first = first + weight * jnp.sum(wide, axis=0)
+        second = second + weight * jnp.sum(wide * wide, axis=0)
+        return first, second
 
     def slice_copy(b, i, first, size):
         other = lax.rem(me + i, n)
@@ -162,8 +171,10 @@
             lax.fori_loop(first, end, first_slot, 0)
             send_slices(0, first, end - first)
     own_copy(0).start()
-    second = lax.fori_loop(0, slots, add_slot, jnp.zeros((group, channels), F32))
-    sums[me, slots : slots + 1, :] = jnp.sum(second, axis=0, keepdims=True)
+    nothing = jnp.zeros((group, channels), F32)
+    first, second = lax.fori_loop(0, slots, add_slot, (nothing, nothing))
+    sums[me, 0:1, :] = jnp.sum(first, axis=0, keepdims=True)
+    sums[me, 1:2, :] = jnp.sum(second, axis=0, keepdims=True)
     lax.fori_loop(1, n, start_moment, 0)
     for b in range(1, blocks):
         build_table(b)
@@ -176,10 +187,10 @@
         send_slices(b, 0, slots)
         own_copy(b).start()
 
-    late = (blocks - 1) * lines
-    back_table[...] = table[late:].T
+    split = (blocks - 1) * lines
+    back_table[...] = table[split:].T
     if blocks > 1:
-        front[...] = table[:late].T
+        front[...] = table[:split].T
     legendre_copy.wait()
     gain_copy.wait()
     row = lax.broadcasted_iota(jnp.int32, (everything, live_total), 0)
@@ -199,23 +210,35 @@
     degree = lax.broadcasted_iota(jnp.int32, (degrees, channels), 0)
     lax.fori_loop(1, n, wait_moment, 0)
     totals = jnp.sum(sums[...], axis=0)
-    mean = jnp.sum(totals[0:slots], axis=0, keepdims=True) / points
-    variance = totals[slots : slots + 1] / points - mean * mean
+    mean = totals[0:1] / points
+    variance = totals[1:2] / points - mean * mean
     gain[...] = gain[...] * lax.rsqrt(variance + 1e-05)
-    for i in range(n):
-        rows[i * slots : (i + 1) * slots, :] = sums[i, 0:slots, :]
-    level = float(np.asarray(1.0 / math.sqrt(longitudes)).astype(BF16))
-
-    def landing(b):
-        return early.at[b, me] if b < blocks - 1 else last.at[me]
-
-    def return_copy(b, i):
+    cuts = sorted({0, (ready + 1) // 2, ready, slots})
+    pieces = [(b, 0, slots) for b in range(blocks - 1)]
+    pieces += [(blocks - 1, first, end) for first, end in zip(cuts[:-1], cuts[1:])]
+
+    def landing(p):
+        b, first, end = pieces[p]
+        if b < blocks - 1:
+            return early.at[b, me]
+        if first < ready:
+            return late.at[me, pl.ds(first, end - first)]
+        return last.at[me]
+
+    def leaving(p, other):
+        b, first, end = pieces[p]
+        return outgoing.at[b, other, pl.ds(first, end - first)]
+
+    def return_copy(p, i):
         other = lax.rem(me + i, n)
         return pltpu.make_async_remote_copy(
-            src_ref=outgoing.at[b, other], dst_ref=landing(b),
-            send_sem=back_send.at[b, i], recv_sem=back_arrive.at[b, i],
+            src_ref=leaving(p, other), dst_ref=landing(p),
+            send_sem=back_send.at[p, i], recv_sem=back_arrive.at[p, i],
             device_id={axis: other}, device_id_type=pl.DeviceIdType.MESH,
         )
+
+    def return_own(p):
+        return pltpu.make_async_copy(leaving(p, me), landing(p), back_own.at[p])
 
     for b in range(blocks):
         count = min(BLOCK, share - b * BLOCK)
@@ -244,16 +267,20 @@
             expanded = jnp.dot(
                 pick[...].astype(BF16), legendre[b * BLOCK + r], preferred_element_type=F32
             ).astype(BF16)
-            pieces = []
+            flag = jnp.where(wave == 0, 1.0, 0.0).astype(F32)
+            parts = []
             for t in range(2):
                 for h in range(halves):
                     lanes = slice(h * 128, (h + 1) * 128)
                     piece = gathered[h, pl.ds(t * BLOCK + r, everything, stride=2 * BLOCK), :]
                     if t == 0:
-                        piece = jnp.where(wave == 0, rows[:, lanes] * level, piece)
+                        rest = gathered[h, pl.ds(BLOCK + r, everything, stride=2 * BLOCK), :]
+                        piece = piece + rest * flag
+                    else:
+                        piece = piece * (1.0 - flag)
                     piece = piece - mean[:, lanes] * row_sum[t * waves + wave]
-                    pieces.append((piece * quad_slot[...]).astype(BF16))
-            weighted = jnp.concatenate(pieces, axis=1)
+                    parts.append((piece * quad_slot[...]).astype(BF16))
+            weighted = jnp.concatenate(parts, axis=1)
             coefficient = lax.dot_general(
                 expanded, weighted, (((0,), (0,)), ((), ())), preferred_element_type=F32
             )
@@ -287,46 +314,71 @@
 
         lax.fori_loop(0, n, narrow, 0)
 
-        def start_return(i, carry):
-            return_copy(b, i).start()
-            return carry
-
-        lax.fori_loop(1, n, start_return, 0)
-        pltpu.make_async_copy(outgoing.at[b, me], landing(b), back_own.at[b]).start()
-
-    def settle(b):
+        for p in range(len(pieces)):
+            if pieces[p][0] == b:
+
+                def start_return(i, carry):
+                    return_copy(p, i).start()
+                    return carry
+
+                lax.fori_loop(1, n, start_return, 0)
+                return_own(p).start()
+
+    def settle(p):
         def wait_return(i, carry):
-            return_copy(b, i).wait()
+            return_copy(p, i).wait()
             return carry
 
         lax.fori_loop(1, n, wait_return, 0)
-        pltpu.make_async_copy(outgoing.at[b, me], landing(b), back_own.at[b]).wait()
-
-    for b in range(blocks - 1):
-        settle(b)
-
-    def partial_slot(s, carry):
-        if blocks > 1:
-            block = early[:, :, s].reshape(late, channels)
-            partial[s] = jnp.dot(front[...], block, preferred_element_type=F32).astype(BF16)
-        else:
-            partial[s] = jnp.zeros(partial.shape[1:], BF16)
-        return carry
-
-    lax.fori_loop(0, slots, partial_slot, 0)
-    settle(blocks - 1)
+        return_own(p).wait()
+
+    def front_part(s):
+        if blocks == 1:
+            return jnp.zeros(partial.shape[1:], F32)
+        block = early[:, :, s].reshape(split, channels)
+        return jnp.dot(front[...], block, preferred_element_type=F32)
+
+    def front_slot(s, carry):
+        partial[s] = front_part(s).astype(BF16)
+        return carry
+
+    def whole_slot(s, carry):
+        block = late[:, s].reshape(lines, channels)
+        total = jnp.dot(back_table[...], block, preferred_element_type=F32)
+        partial[s] = (front_part(s) + total).astype(BF16)
+        return carry
+
+    for p in range(blocks - 1):
+        settle(p)
+    lax.fori_loop(ready, slots, front_slot, 0)
+    for p in range(blocks - 1, len(pieces)):
+        settle(p)
+        if pieces[p][1] < ready:
+            lax.fori_loop(pieces[p][1], pieces[p][2], whole_slot, 0)
 
 
 def inverse_kernel(last, table, partial, out, held, store):
     slots = partial.shape[0]
+    ready = slots - last.shape[1]
+
+    def store_ready(s):
+        return pltpu.make_async_copy(partial.at[s], out.at[s], store.at[s])
 
     def store_slot(s):
-        return pltpu.make_async_copy(held.at[s], out.at[s], store.at[s])
+        return pltpu.make_async_copy(held.at[s], out.at[ready + s], store.at[ready + s])
+
+    def start_ready(s, carry):
+        store_ready(s).start()
+        return carry
+
+    def wait_ready(s, carry):
+        store_ready(s).wait()
+        return carry
 
     def finish_slot(s, carry):
         block = last[:, s].reshape(table.shape[1], last.shape[-1])
         total = jnp.dot(table[...], block, preferred_element_type=F32)
-        held[s] = (partial[s].astype(F32) + total).astype(BF16)
+        held[s] = (partial[ready + s].astype(F32) + total).astype(BF16)
         store_slot(s).start()
         return carry
 
@@ -334,8 +386,10 @@
         store_slot(s).wait()
         return carry
 
-    lax.fori_loop(0, slots, finish_slot, 0)
-    lax.fori_loop(0, slots, wait_store, 0)
+    lax.fori_loop(0, ready, start_ready, 0)
+    lax.fori_loop(0, slots - ready, finish_slot, 0)
+    lax.fori_loop(0, ready, wait_ready, 0)
+    lax.fori_loop(0, slots - ready, wait_store, 0)
 
 
 def body(
@@ -358,18 +412,20 @@
     packet = (blocks, n, slots, 2 * BLOCK, channels)
     copies = pltpu.SemaphoreType.DMA
     lines = n * 2 * BLOCK
+    tail = min(TAIL, slots)
+    returns = blocks + 2
     last, back_table, partial = pl.pallas_call(
         functools.partial(spectral_kernel, "lat", n, live_total * longitudes, share),
         out_shape=(
-            pltpu.VMEM(packet[1:], BF16),
+            pltpu.VMEM((n, tail) + packet[3:], BF16),
             pltpu.VMEM((longitudes, lines), BF16),
             pltpu.VMEM((slots, longitudes, channels), BF16),
         ),
         in_specs=[smem, smem, smem, anywhere, anywhere, anywhere, vmem, anywhere, vmem],
         out_specs=(vmem, vmem, vmem),
         scratch_shapes=[
-            pltpu.VMEM((n, slots + 1, channels), F32),
-            pltpu.VMEM((everything, channels), F32),
+            pltpu.VMEM((n, 2, channels), F32),
+            pltpu.VMEM((n * padded, channels), F32),
             pltpu.VMEM((n * padded, waves), F32),
             pltpu.VMEM((blocks * lines, longitudes), BF16),
             pltpu.VMEM((longitudes, max(blocks - 1, 1) * lines), BF16),
@@ -381,13 +437,14 @@
             pltpu.VMEM(packet, BF16),
             pltpu.VMEM((channels // 128, everything * 2 * BLOCK, 128), F32),
             pltpu.VMEM((max(blocks - 1, 1),) + packet[1:], BF16),
+            pltpu.VMEM((n, max(slots - tail, 1)) + packet[3:], BF16),
             pltpu.VMEM(base.shape, BF16),
             pltpu.VMEM(legendre.shape, BF16),
             pltpu.VMEM(spectral_gain.shape, F32),
             copies((slots,)), copies((3,)),
             copies((n,)), copies((n,)),
             copies((blocks, n)), copies((blocks, n)), copies((blocks,)),
-            copies((blocks, n)), copies((blocks, n)), copies((blocks,)),
+            copies((returns, n)), copies((returns, n)), copies((returns,)),
         ],
         compiler_params=pltpu.CompilerParams(
             collective_id=0, has_side_effects=True, vmem_limit_bytes=limit
@@ -403,7 +460,7 @@
         in_specs=[vmem, vmem, vmem],
         out_specs=anywhere,
         scratch_shapes=[
-            pltpu.VMEM((slots, longitudes, channels), BF16),
+            pltpu.VMEM((tail, longitudes, channels), BF16),
             copies((slots,)),
         ],
         compiler_params=pltpu.CompilerParams(vmem_limit_bytes=16 * 1024 * 1024),

time: 133 us -> 137 us (1.030); the launches traced: 133 us -> 135 us
  local copies, waits for them, and re-layouts: 0 us -> 3.58 us
    unnamed x0 -> x10, local copies, waits for them, and re-layouts: none -> 3.58 us
where the time goes in v2:
time: 137 us; the launch traced here: 135 us
  Pallas kernels  132 us (96%)
  local copies, waits for them, and re-layouts  3.58 us (3%)
    pallas_call x1, Pallas kernels, body(): pl.pallas_call(functools.partial(spectral_kernel, 'lat', n, live_total *...  129 us
    unnamed x10, local copies, waits for them, and re-layouts  3.58 us

profile of v2, /device:TPU:13, one launch (start us, length us, event | category | flops | bytes accessed | tf_op | source)
XLA Modules:
  0.0 135.3 jit_solution(9390102357757991514)
XLA Ops:
  0.0 0.0 copy-start
  0.0 0.9 copy-done
  0.9 0.0 copy-start.1
  0.9 0.7 copy-done.1
  1.6 0.0 copy-start.2
  1.6 0.7 copy-done.2
  2.3 0.0 copy-start.3
  2.3 0.7 copy-done.3
  2.9 0.0 copy-start.4
  2.9 0.7 copy-done.4
  3.6 129.4 %shard_map.91 = (bf16[16,1,16,256]{3,2,1,0:T(8,128)(2,1)S(1)}, bf16[1440,256]{1,0:T(8,128)(2,1)S(1)}, bf16[7,1440,256]{2,1,0:T(8,128)(2,1)S(1)}) custom-call(s32[16]{0:T(128)S(1)} %copy-done.3, s32[384]{0:T(512)S(1)} %copy-done.2, f32[768]{0:T(1024)S(1)} %copy-done.1, bf16[7,1440,256]{2,1,0:T(8,128)(2,1)} %x.1, bf16[768,1440]{1,0:T(8,128)(2,1)} %constant.4.clone.base_far, ...), custom_call_target="tpu_custom_call" | custom-call | tf_op jit(solution)/shard_map/pallas_call | solution.py:417
  132.9 2.4 %shard_map.92 = bf16[7,1440,256]{2,1,0:T(8,128)(2,1)} custom-call(bf16[16,1,16,256]{3,2,1,0:T(8,128)(2,1)S(1)} %get-tuple-element.8.last, bf16[1440,256]{1,0:T(8,128)(2,1)S(1)} %get-tuple-element.9.table, bf16[7,1440,256]{2,1,0:T(8,128)(2,1)S(1)} %get-tuple-element.10.partial), custom_call_target="tpu_custom_call" | custom-call | tf_op jit(solution)/shard_map/pallas_call | solution.py:457
Async XLA Ops:
  0.0 0.9 copy-start
  0.9 0.7 copy-start.1
  1.6 0.7 copy-start.2
  2.3 0.7 copy-start.3
  2.9 0.7 copy-start.4

commit v3 on v2

--- a/solution.py
+++ b/solution.py
@@ -38,9 +38,9 @@
 
 
 def spectral_kernel(
-    axis, n, points, share, counts, owner, row_sum, x, base_far, legendre_far, quad, gain_far,
-    mix, last, back_table, partial,
-    sums, zero, hot, table, front, spec, recv, gathered, pick, quad_slot, outgoing, result,
+    axis, n, points, share, counts_far, owner_far, row_sum_far, x, base_far, legendre_far,
+    quad_far, gain_far, mix_far, last, back_table, partial,
+    counts, owner, row_sum, quad, mix, sums, zero, hot, table, front, spec, recv, gathered, pick, quad_slot, outgoing, result,
     early, late, base, legendre, gain,
     load, fetch, mom_send, mom_recv, send, arrive, own, back_send, back_arrive, back_own,
 ):
@@ -64,8 +64,18 @@
     base_copy = pltpu.make_async_copy(base_far, base, fetch.at[0])
     legendre_copy = pltpu.make_async_copy(legendre_far, legendre, fetch.at[1])
     gain_copy = pltpu.make_async_copy(gain_far, gain, fetch.at[2])
+    owner_copy = pltpu.make_async_copy(owner_far, owner, fetch.at[3])
+    counts_copy = pltpu.make_async_copy(counts_far, counts, fetch.at[4])
+    row_sum_copy = pltpu.make_async_copy(row_sum_far, row_sum, fetch.at[5])
+    quad_copy = pltpu.make_async_copy(quad_far, quad, fetch.at[6])
+    mix_copy = pltpu.make_async_copy(mix_far, mix, fetch.at[7])
+    owner_copy.start()
     base_copy.start()
     lax.fori_loop(0, slots, start_load, 0)
+    counts_copy.start()
+    row_sum_copy.start()
+    quad_copy.start()
+    mix_copy.start()
     legendre_copy.start()
     gain_copy.start()
     barrier = greet_all(axis, n, me)
@@ -83,8 +93,10 @@
             hot[pl.ds(begin, BLOCK), :] = jnp.where(lane_of == held, 1.0, 0.0).astype(F32)
         return carry
 
+    owner_copy.wait()
     lax.fori_loop(0, n, choose_rows, 0)
     zero[...] = jnp.broadcast_to(hot[:, 0:1], zero.shape)
+    counts_copy.wait()
     live = counts[me]
     group = math.gcd(longitudes, 32)
 
@@ -193,6 +205,9 @@
         front[...] = table[:split].T
     legendre_copy.wait()
     gain_copy.wait()
+    row_sum_copy.wait()
+    quad_copy.wait()
+    mix_copy.wait()
     row = lax.broadcasted_iota(jnp.int32, (everything, live_total), 0)
     lane = lax.broadcasted_iota(jnp.int32, (everything, live_total), 1)
     pick[...] = jnp.zeros_like(pick)
@@ -406,9 +421,9 @@
     row_sum = jnp.asarray(trig.astype(np.float64).sum(axis=1).astype(np.float32))
 
     vmem = pl.BlockSpec(memory_space=pltpu.VMEM)
-    smem = pl.BlockSpec(memory_space=pltpu.SMEM)
     anywhere = pl.BlockSpec(memory_space=pl.ANY)
     limit = 48 * 1024 * 1024
+    far = functools.partial(pltpu.with_memory_space_constraint, memory_space=pltpu.HBM)
     packet = (blocks, n, slots, 2 * BLOCK, channels)
     copies = pltpu.SemaphoreType.DMA
     lines = n * 2 * BLOCK
@@ -421,9 +436,14 @@
             pltpu.VMEM((longitudes, lines), BF16),
             pltpu.VMEM((slots, longitudes, channels), BF16),
         ),
-        in_specs=[smem, smem, smem, anywhere, anywhere, anywhere, vmem, anywhere, vmem],
+        in_specs=[anywhere] * 9,
         out_specs=(vmem, vmem, vmem),
         scratch_shapes=[
+            pltpu.SMEM(lat_counts.shape, jnp.int32),
+            pltpu.SMEM(owner_wavenumber.shape, jnp.int32),
+            pltpu.SMEM(row_sum.shape, F32),
+            pltpu.VMEM((1, live_total), F32),
+            pltpu.VMEM(channel_mix.shape, BF16),
             pltpu.VMEM((n, 2, channels), F32),
             pltpu.VMEM((n * padded, channels), F32),
             pltpu.VMEM((n * padded, waves), F32),
@@ -441,7 +461,7 @@
             pltpu.VMEM(base.shape, BF16),
             pltpu.VMEM(legendre.shape, BF16),
             pltpu.VMEM(spectral_gain.shape, F32),
-            copies((slots,)), copies((3,)),
+            copies((slots,)), copies((8,)),
             copies((n,)), copies((n,)),
             copies((blocks, n)), copies((blocks, n)), copies((blocks,)),
             copies((returns, n)), copies((returns, n)), copies((returns,)),
@@ -450,8 +470,10 @@
             collective_id=0, has_side_effects=True, vmem_limit_bytes=limit
         ),
     )(
-        lat_counts, owner_wavenumber, row_sum, grid_values, base, legendre,
-        quad_weight.reshape(1, live_total), spectral_gain, channel_mix,
+        *map(far, (
+            lat_counts, owner_wavenumber, row_sum, grid_values, base, legendre,
+            quad_weight.reshape(1, live_total), spectral_gain, channel_mix,
+        ))
     )
 
     return pl.pallas_call(

time: 137 us -> 132 us (0.964)
  local copies, waits for them, and re-layouts: 3.58 us -> 0 us
    unnamed x10 -> x0, local copies, waits for them, and re-layouts: 3.58 us -> none
where the time goes in v3:
time: 132 us; the launch traced here: 131 us
  Pallas kernels  131 us (99%)
    pallas_call x1, Pallas kernels, body(): pl.pallas_call(functools.partial(spectral_kernel, 'lat', n, live_total *...  129 us

profile of v3, /device:TPU:13, one launch (start us, length us, event | category | flops | bytes accessed | tf_op | source)
XLA Modules:
  0.0 131.1 jit_solution(1776668189793666193)
XLA Ops:
  0.0 128.8 %shard_map.91 = (bf16[16,1,16,256]{3,2,1,0:T(8,128)(2,1)S(1)}, bf16[1440,256]{1,0:T(8,128)(2,1)S(1)}, bf16[7,1440,256]{2,1,0:T(8,128)(2,1)S(1)}) custom-call(s32[16]{0:T(128)} %counts_far.1, s32[384]{0:T(512)} %owner_far.1, f32[768]{0:T(1024)} %constant.5.clone.row_sum_far, bf16[7,1440,256]{2,1,0:T(8,128)(2,1)} %x.1, ...), custom_call_target="tpu_custom_call" | custom-call | tf_op jit(solution)/shard_map/pallas_call | solution.py:432
  128.8 2.4 %shard_map.92 = bf16[7,1440,256]{2,1,0:T(8,128)(2,1)} custom-call(bf16[16,1,16,256]{3,2,1,0:T(8,128)(2,1)S(1)} %get-tuple-element.8.last, bf16[1440,256]{1,0:T(8,128)(2,1)S(1)} %get-tuple-element.9.table, bf16[7,1440,256]{2,1,0:T(8,128)(2,1)S(1)} %get-tuple-element.10.partial), custom_call_target="tpu_custom_call" | custom-call | tf_op jit(solution)/shard_map/pallas_call | solution.py:479

commit v4 on v3

--- a/solution.py
+++ b/solution.py
@@ -10,7 +10,7 @@
 from jax.sharding import PartitionSpec as P
 
 BLOCK = 8
-TAIL = 1
+FIRST = 2
 F32 = jnp.float32
 BF16 = jnp.bfloat16
 
@@ -41,7 +41,7 @@
     axis, n, points, share, counts_far, owner_far, row_sum_far, x, base_far, legendre_far,
     quad_far, gain_far, mix_far, last, back_table, partial,
     counts, owner, row_sum, quad, mix, sums, zero, hot, table, front, spec, recv, gathered, pick, quad_slot, outgoing, result,
-    early, late, base, legendre, gain,
+    early, base, legendre, gain,
     load, fetch, mom_send, mom_recv, send, arrive, own, back_send, back_arrive, back_own,
 ):
     me = lax.axis_index(axis)
@@ -52,7 +52,6 @@
     blocks = spec.shape[0]
     lines = n * 2 * BLOCK
     waves = base.shape[0] // 2
-    ready = slots - last.shape[1]
 
     def load_slot(s):
         return pltpu.make_async_copy(x.at[s], partial.at[s], load.at[s])
@@ -167,21 +166,19 @@
 
     base_copy.wait()
     build_table(0)
-    load_slot(0).wait()
-    transform(0, 0)
-    pl.semaphore_wait(barrier, n - 1)
-    send_slices(0, 0, 1)
 
     def first_slot(s, carry):
         load_slot(s).wait()
         transform(0, s)
         return carry
 
-    cuts = [1, 1 + (slots - 1) // 3, slots]
-    for first, end in zip(cuts[:-1], cuts[1:]):
-        if end > first:
-            lax.fori_loop(first, end, first_slot, 0)
-            send_slices(0, first, end - first)
+    opening = min(FIRST, slots)
+    lax.fori_loop(0, opening, first_slot, 0)
+    pl.semaphore_wait(barrier, n - 1)
+    send_slices(0, 0, opening)
+    if opening < slots:
+        lax.fori_loop(opening, slots, first_slot, 0)
+        send_slices(0, opening, slots - opening)
     own_copy(0).start()
     nothing = jnp.zeros((group, channels), F32)
     first, second = lax.fori_loop(0, slots, add_slot, (nothing, nothing))
@@ -228,32 +225,19 @@
     mean = totals[0:1] / points
     variance = totals[1:2] / points - mean * mean
     gain[...] = gain[...] * lax.rsqrt(variance + 1e-05)
-    cuts = sorted({0, (ready + 1) // 2, ready, slots})
-    pieces = [(b, 0, slots) for b in range(blocks - 1)]
-    pieces += [(blocks - 1, first, end) for first, end in zip(cuts[:-1], cuts[1:])]
-
-    def landing(p):
-        b, first, end = pieces[p]
-        if b < blocks - 1:
-            return early.at[b, me]
-        if first < ready:
-            return late.at[me, pl.ds(first, end - first)]
-        return last.at[me]
-
-    def leaving(p, other):
-        b, first, end = pieces[p]
-        return outgoing.at[b, other, pl.ds(first, end - first)]
-
-    def return_copy(p, i):
+    def landing(b):
+        return early.at[b, me] if b < blocks - 1 else last.at[me]
+
+    def return_copy(b, i):
         other = lax.rem(me + i, n)
         return pltpu.make_async_remote_copy(
-            src_ref=leaving(p, other), dst_ref=landing(p),
-            send_sem=back_send.at[p, i], recv_sem=back_arrive.at[p, i],
+            src_ref=outgoing.at[b, other], dst_ref=landing(b),
+            send_sem=back_send.at[b, i], recv_sem=back_arrive.at[b, i],
             device_id={axis: other}, device_id_type=pl.DeviceIdType.MESH,
         )
 
-    def return_own(p):
-        return pltpu.make_async_copy(leaving(p, me), landing(p), back_own.at[p])
+    def return_own(b):
+        return pltpu.make_async_copy(outgoing.at[b, me], landing(b), back_own.at[b])
 
     for b in range(blocks):
         count = min(BLOCK, share - b * BLOCK)
@@ -329,82 +313,48 @@
 
         lax.fori_loop(0, n, narrow, 0)
 
-        for p in range(len(pieces)):
-            if pieces[p][0] == b:
-
-                def start_return(i, carry):
-                    return_copy(p, i).start()
-                    return carry
-
-                lax.fori_loop(1, n, start_return, 0)
-                return_own(p).start()
-
-    def settle(p):
+        def start_return(i, carry):
+            return_copy(b, i).start()
+            return carry
+
+        lax.fori_loop(1, n, start_return, 0)
+        return_own(b).start()
+
+    def settle(b):
         def wait_return(i, carry):
-            return_copy(p, i).wait()
+            return_copy(b, i).wait()
             return carry
 
         lax.fori_loop(1, n, wait_return, 0)
-        return_own(p).wait()
-
-    def front_part(s):
-        if blocks == 1:
-            return jnp.zeros(partial.shape[1:], F32)
-        block = early[:, :, s].reshape(split, channels)
-        return jnp.dot(front[...], block, preferred_element_type=F32)
-
-    def front_slot(s, carry):
-        partial[s] = front_part(s).astype(BF16)
-        return carry
-
-    def whole_slot(s, carry):
-        block = late[:, s].reshape(lines, channels)
-        total = jnp.dot(back_table[...], block, preferred_element_type=F32)
-        partial[s] = (front_part(s) + total).astype(BF16)
-        return carry
-
-    for p in range(blocks - 1):
-        settle(p)
-    lax.fori_loop(ready, slots, front_slot, 0)
-    for p in range(blocks - 1, len(pieces)):
-        settle(p)
-        if pieces[p][1] < ready:
-            lax.fori_loop(pieces[p][1], pieces[p][2], whole_slot, 0)
+        return_own(b).wait()
+
+    def partial_slot(s, carry):
+        if blocks > 1:
+            block = early[:, :, s].reshape(split, channels)
+            partial[s] = jnp.dot(front[...], block, preferred_element_type=F32).astype(BF16)
+        else:
+            partial[s] = jnp.zeros(partial.shape[1:], BF16)
+        return carry
+
+    for b in range(blocks - 1):
+        settle(b)
+    lax.fori_loop(0, slots, partial_slot, 0)
+    settle(blocks - 1)
 
 
 def inverse_kernel(last, table, partial, out, held, store):
     slots = partial.shape[0]
-    ready = slots - last.shape[1]
-
-    def store_ready(s):
-        return pltpu.make_async_copy(partial.at[s], out.at[s], store.at[s])
 
     def store_slot(s):
-        return pltpu.make_async_copy(held.at[s], out.at[ready + s], store.at[ready + s])
-
-    def start_ready(s, carry):
-        store_ready(s).start()
-        return carry
-
-    def wait_ready(s, carry):
-        store_ready(s).wait()
-        return carry
-
-    def finish_slot(s, carry):
+        return pltpu.make_async_copy(held.at[s], out.at[s], store.at[s])
+
+    for s in range(slots):
         block = last[:, s].reshape(table.shape[1], last.shape[-1])
         total = jnp.dot(table[...], block, preferred_element_type=F32)
-        held[s] = (partial[ready + s].astype(F32) + total).astype(BF16)
+        held[s] = (partial[s].astype(F32) + total).astype(BF16)
         store_slot(s).start()
-        return carry
-
-    def wait_store(s, carry):
+    for s in range(slots):
         store_slot(s).wait()
-        return carry
-
-    lax.fori_loop(0, ready, start_ready, 0)
-    lax.fori_loop(0, slots - ready, finish_slot, 0)
-    lax.fori_loop(0, ready, wait_ready, 0)
-    lax.fori_loop(0, slots - ready, wait_store, 0)
 
 
 def body(
@@ -427,12 +377,10 @@
     packet = (blocks, n, slots, 2 * BLOCK, channels)
     copies = pltpu.SemaphoreType.DMA
     lines = n * 2 * BLOCK
-    tail = min(TAIL, slots)
-    returns = blocks + 2
     last, back_table, partial = pl.pallas_call(
         functools.partial(spectral_kernel, "lat", n, live_total * longitudes, share),
         out_shape=(
-            pltpu.VMEM((n, tail) + packet[3:], BF16),
+            pltpu.VMEM(packet[1:], BF16),
             pltpu.VMEM((longitudes, lines), BF16),
             pltpu.VMEM((slots, longitudes, channels), BF16),
         ),
@@ -457,14 +405,13 @@
             pltpu.VMEM(packet, BF16),
             pltpu.VMEM((channels // 128, everything * 2 * BLOCK, 128), F32),
             pltpu.VMEM((max(blocks - 1, 1),) + packet[1:], BF16),
-            pltpu.VMEM((n, max(slots - tail, 1)) + packet[3:], BF16),
             pltpu.VMEM(base.shape, BF16),
             pltpu.VMEM(legendre.shape, BF16),
             pltpu.VMEM(spectral_gain.shape, F32),
             copies((slots,)), copies((8,)),
             copies((n,)), copies((n,)),
             copies((blocks, n)), copies((blocks, n)), copies((blocks,)),
-            copies((returns, n)), copies((returns, n)), copies((returns,)),
+            copies((blocks, n)), copies((blocks, n)), copies((blocks,)),
         ],
         compiler_params=pltpu.CompilerParams(
             collective_id=0, has_side_effects=True, vmem_limit_bytes=limit
@@ -482,7 +429,7 @@
         in_specs=[vmem, vmem, vmem],
         out_specs=anywhere,
         scratch_shapes=[
-            pltpu.VMEM((tail, longitudes, channels), BF16),
+            pltpu.VMEM((slots, longitudes, channels), BF16),
             copies((slots,)),
         ],
         compiler_params=pltpu.CompilerParams(vmem_limit_bytes=16 * 1024 * 1024),

time: 132 us -> 130 us (0.985)
  Pallas kernels: 131 us -> 129 us
    pallas_call x1, Pallas kernels: 129 us -> 127 us  [body(): pl.pallas_call(functools.partial(spectral_kernel, 'lat', n, live_total *...]
where the time goes in v4:
time: 130 us; the launch traced here: 129 us
  Pallas kernels  129 us (99%)
    pallas_call x1, Pallas kernels, body(): pl.pallas_call(functools.partial(spectral_kernel, 'lat', n, live_total *...  127 us
    pallas_call x1, Pallas kernels, body(): pl.pallas_call(inverse_kernel, out_shape=jax.ShapeDtypeStruct((slots, lon...  2.88 us

profile of v4, /device:TPU:13, one launch (start us, length us, event | category | flops | bytes accessed | tf_op | source)
XLA Modules:
  0.0 129.5 jit_solution(4455981050698110160)
XLA Ops:
  0.0 126.6 %shard_map.91 = (bf16[16,7,16,256]{3,2,1,0:T(8,128)(2,1)S(1)}, bf16[1440,256]{1,0:T(8,128)(2,1)S(1)}, bf16[7,1440,256]{2,1,0:T(8,128)(2,1)S(1)}) custom-call(s32[16]{0:T(128)} %counts_far.1, s32[384]{0:T(512)} %owner_far.1, f32[768]{0:T(1024)} %constant.5.clone.row_sum_far, bf16[7,1440,256]{2,1,0:T(8,128)(2,1)} %x.1, ...), custom_call_target="tpu_custom_call" | custom-call | tf_op jit(solution)/shard_map/pallas_call | solution.py:380
  126.6 2.9 %shard_map.92 = bf16[7,1440,256]{2,1,0:T(8,128)(2,1)} custom-call(bf16[16,7,16,256]{3,2,1,0:T(8,128)(2,1)S(1)} %get-tuple-element.8.last, bf16[1440,256]{1,0:T(8,128)(2,1)S(1)} %get-tuple-element.9.table, bf16[7,1440,256]{2,1,0:T(8,128)(2,1)S(1)} %get-tuple-element.10.partial), custom_call_target="tpu_custom_call" | custom-call | tf_op jit(solution)/shard_map/pallas_call | solution.py:426

commit v5 on v4

--- a/solution.py
+++ b/solution.py
@@ -11,6 +11,8 @@
 
 BLOCK = 8
 FIRST = 2
+TAIL = 3
+HELD = 1
 F32 = jnp.float32
 BF16 = jnp.bfloat16
 
@@ -23,6 +25,14 @@
     return table.astype(BF16)
 
 
+def homeward_pieces(blocks, slots, ready, held_back):
+    pieces = [(b, 1, 0, slots) for b in range(held_back)]
+    if ready > 0:
+        pieces.append((held_back, blocks - held_back, 0, ready))
+    pieces.append((held_back, blocks - held_back, ready, slots - ready))
+    return pieces
+
+
 def greet_all(axis, count, me):
     barrier = pltpu.get_barrier_semaphore()
 
@@ -40,8 +50,8 @@
 def spectral_kernel(
     axis, n, points, share, counts_far, owner_far, row_sum_far, x, base_far, legendre_far,
     quad_far, gain_far, mix_far, last, back_table, partial,
-    counts, owner, row_sum, quad, mix, sums, zero, hot, table, front, spec, recv, gathered, pick, quad_slot, outgoing, result,
-    early, base, legendre, gain,
+    counts, owner, row_sum, quad, mix, halves_of, sums, zero, hot, table, front, spec, recv, gathered, pick, quad_slot, outgoing, result,
+    back, base, legendre, gain,
     load, fetch, mom_send, mom_recv, send, arrive, own, back_send, back_arrive, back_own,
 ):
     me = lax.axis_index(axis)
@@ -52,6 +62,8 @@
     blocks = spec.shape[0]
     lines = n * 2 * BLOCK
     waves = base.shape[0] // 2
+    ready, held_back = slots - last.shape[2], blocks - last.shape[0]
+    homeward = homeward_pieces(blocks, slots, ready, held_back)
 
     def load_slot(s):
         return pltpu.make_async_copy(x.at[s], partial.at[s], load.at[s])
@@ -69,34 +81,31 @@
     quad_copy = pltpu.make_async_copy(quad_far, quad, fetch.at[6])
     mix_copy = pltpu.make_async_copy(mix_far, mix, fetch.at[7])
     owner_copy.start()
+    opening = min(FIRST, slots)
     base_copy.start()
-    lax.fori_loop(0, slots, start_load, 0)
-    counts_copy.start()
-    row_sum_copy.start()
-    quad_copy.start()
-    mix_copy.start()
-    legendre_copy.start()
-    gain_copy.start()
+    lax.fori_loop(0, opening, start_load, 0)
     barrier = greet_all(axis, n, me)
 
     row_of = lax.broadcasted_iota(jnp.int32, (BLOCK, waves), 0)
     lane_of = lax.broadcasted_iota(jnp.int32, (BLOCK, waves), 1)
 
-    def choose_rows(o, carry):
-        for b in range(blocks):
-            count = min(BLOCK, share - b * BLOCK)
+    def choose_rows(b):
+        count = min(BLOCK, share - b * BLOCK)
+
+        def choose_owner(o, carry):
             held = jnp.full((BLOCK, waves), -1, jnp.int32)
             for r in range(count):
                 held = jnp.where(row_of == r, owner[o * share + b * BLOCK + r], held)
             begin = pl.multiple_of((b * n + o) * BLOCK, BLOCK)
-            hot[pl.ds(begin, BLOCK), :] = jnp.where(lane_of == held, 1.0, 0.0).astype(F32)
-        return carry
+            hit = jnp.where(lane_of == held, 1.0, 0.0).astype(F32)
+            hot[pl.ds(begin, BLOCK), :] = hit
+            zero[pl.ds(begin, BLOCK), :] = jnp.broadcast_to(hit[:, 0:1], (BLOCK, channels))
+            return carry
+
+        lax.fori_loop(0, n, choose_owner, 0)
 
     owner_copy.wait()
-    lax.fori_loop(0, n, choose_rows, 0)
-    zero[...] = jnp.broadcast_to(hot[:, 0:1], zero.shape)
-    counts_copy.wait()
-    live = counts[me]
+    choose_rows(0)
     group = math.gcd(longitudes, 32)
 
     def build_table(b):
@@ -118,7 +127,7 @@
         out = jnp.concatenate([real, imag], axis=1)
         spec[b, :, s] = out.astype(BF16)
 
-    def add_slot(s, carry):
+    def add_slot(live, s, carry):
         first, second = carry
         wide = partial[s].astype(F32).reshape(-1, group, channels)
         weight = jnp.where(s < live, 1.0, 0.0).astype(F32)
@@ -145,10 +154,20 @@
 
         lax.fori_loop(1, n, start_slices, 0)
 
+    pairs, pair = n // 2, me // 2
+
+    def partner_copy():
+        return pltpu.make_async_remote_copy(
+            src_ref=halves_of.at[0], dst_ref=halves_of.at[1],
+            send_sem=mom_send.at[0], recv_sem=mom_recv.at[0],
+            device_id={axis: me + 1 - 2 * lax.rem(me, 2)},
+            device_id_type=pl.DeviceIdType.MESH,
+        )
+
     def moment_copy(i):
-        other = lax.rem(me + i, n)
+        other = lax.rem(me + 2 * i, n)
         return pltpu.make_async_remote_copy(
-            src_ref=sums.at[me], dst_ref=sums.at[me],
+            src_ref=sums.at[pair], dst_ref=sums.at[pair],
             send_sem=mom_send.at[i], recv_sem=mom_recv.at[i],
             device_id={axis: other}, device_id_type=pl.DeviceIdType.MESH,
         )
@@ -165,6 +184,13 @@
         return pltpu.make_async_copy(spec.at[b, me], recv.at[b, me], own.at[b])
 
     base_copy.wait()
+    lax.fori_loop(opening, slots, start_load, 0)
+    counts_copy.start()
+    row_sum_copy.start()
+    quad_copy.start()
+    mix_copy.start()
+    legendre_copy.start()
+    gain_copy.start()
     build_table(0)
 
     def first_slot(s, carry):
@@ -172,7 +198,6 @@
         transform(0, s)
         return carry
 
-    opening = min(FIRST, slots)
     lax.fori_loop(0, opening, first_slot, 0)
     pl.semaphore_wait(barrier, n - 1)
     send_slices(0, 0, opening)
@@ -180,12 +205,20 @@
         lax.fori_loop(opening, slots, first_slot, 0)
         send_slices(0, opening, slots - opening)
     own_copy(0).start()
+    counts_copy.wait()
+    live = counts[me]
     nothing = jnp.zeros((group, channels), F32)
-    first, second = lax.fori_loop(0, slots, add_slot, (nothing, nothing))
-    sums[me, 0:1, :] = jnp.sum(first, axis=0, keepdims=True)
-    sums[me, 1:2, :] = jnp.sum(second, axis=0, keepdims=True)
-    lax.fori_loop(1, n, start_moment, 0)
+    first, second = lax.fori_loop(
+        0, slots, functools.partial(add_slot, live), (nothing, nothing)
+    )
+    halves_of[0, 0:1, :] = jnp.sum(first, axis=0, keepdims=True)
+    halves_of[0, 1:2, :] = jnp.sum(second, axis=0, keepdims=True)
+    partner_copy().start()
+    partner_copy().wait()
+    sums[pair] = halves_of[0] + halves_of[1]
+    lax.fori_loop(1, pairs, start_moment, 0)
     for b in range(1, blocks):
+        choose_rows(b)
         build_table(b)
 
         def slot_step(s, carry):
@@ -196,10 +229,12 @@
         send_slices(b, 0, slots)
         own_copy(b).start()
 
-    split = (blocks - 1) * lines
-    back_table[...] = table[split:].T
-    if blocks > 1:
-        front[...] = table[:split].T
+    split = held_back * lines
+    for b in range(blocks):
+        turned = table[b * lines : (b + 1) * lines].T
+        front[:, b * lines : (b + 1) * lines] = turned
+        if b >= held_back:
+            back_table[:, (b - held_back) * lines : (b - held_back + 1) * lines] = turned
     legendre_copy.wait()
     gain_copy.wait()
     row_sum_copy.wait()
@@ -220,24 +255,32 @@
         jnp.sum(pick[...] * quad[...], axis=1, keepdims=True), quad_slot.shape
     )
     degree = lax.broadcasted_iota(jnp.int32, (degrees, channels), 0)
-    lax.fori_loop(1, n, wait_moment, 0)
+    lax.fori_loop(1, pairs, wait_moment, 0)
     totals = jnp.sum(sums[...], axis=0)
     mean = totals[0:1] / points
     variance = totals[1:2] / points - mean * mean
     gain[...] = gain[...] * lax.rsqrt(variance + 1e-05)
-    def landing(b):
-        return early.at[b, me] if b < blocks - 1 else last.at[me]
-
-    def return_copy(b, i):
+    def part(ref, piece, device):
+        b, many, first, size = piece
+        return ref.at[pl.ds(b, many), device, pl.ds(first, size)]
+
+    def landing(p):
+        if p < len(homeward) - 1:
+            return part(back, homeward[p], me)
+        return last.at[:, me]
+
+    def return_copy(p, i):
         other = lax.rem(me + i, n)
         return pltpu.make_async_remote_copy(
-            src_ref=outgoing.at[b, other], dst_ref=landing(b),
-            send_sem=back_send.at[b, i], recv_sem=back_arrive.at[b, i],
+            src_ref=part(outgoing, homeward[p], other), dst_ref=landing(p),
+            send_sem=back_send.at[p, i], recv_sem=back_arrive.at[p, i],
             device_id={axis: other}, device_id_type=pl.DeviceIdType.MESH,
         )
 
-    def return_own(b):
-        return pltpu.make_async_copy(outgoing.at[b, me], landing(b), back_own.at[b])
+    def return_own(p):
+        return pltpu.make_async_copy(
+            part(outgoing, homeward[p], me), landing(p), back_own.at[p]
+        )
 
     for b in range(blocks):
         count = min(BLOCK, share - b * BLOCK)
@@ -313,45 +356,61 @@
 
         lax.fori_loop(0, n, narrow, 0)
 
-        def start_return(i, carry):
-            return_copy(b, i).start()
-            return carry
-
-        lax.fori_loop(1, n, start_return, 0)
-        return_own(b).start()
-
-    def settle(b):
+        for p, piece in enumerate(homeward):
+            if piece[0] + piece[1] - 1 == b:
+
+                def start_return(i, carry):
+                    return_copy(p, i).start()
+                    return carry
+
+                lax.fori_loop(1, n, start_return, 0)
+                return_own(p).start()
+
+    def settle(p):
         def wait_return(i, carry):
-            return_copy(b, i).wait()
+            return_copy(p, i).wait()
             return carry
 
         lax.fori_loop(1, n, wait_return, 0)
-        return_own(b).wait()
-
-    def partial_slot(s, carry):
-        if blocks > 1:
-            block = early[:, :, s].reshape(split, channels)
-            partial[s] = jnp.dot(front[...], block, preferred_element_type=F32).astype(BF16)
+        return_own(p).wait()
+
+    def whole_slot(s, carry):
+        block = back[:, :, s].reshape(blocks * lines, channels)
+        partial[s] = jnp.dot(front[...], block, preferred_element_type=F32).astype(BF16)
+        return carry
+
+    def front_slot(s, carry):
+        if held_back > 0:
+            block = back[:held_back, :, s].reshape(split, channels)
+            total = jnp.dot(front[:, :split], block, preferred_element_type=F32)
+            partial[s] = total.astype(BF16)
         else:
             partial[s] = jnp.zeros(partial.shape[1:], BF16)
         return carry
 
-    for b in range(blocks - 1):
-        settle(b)
-    lax.fori_loop(0, slots, partial_slot, 0)
-    settle(blocks - 1)
+    for p in range(held_back):
+        settle(p)
+    lax.fori_loop(ready, slots, front_slot, 0)
+    for p in range(held_back, len(homeward) - 1):
+        settle(p)
+        lax.fori_loop(0, ready, whole_slot, 0)
+    settle(len(homeward) - 1)
 
 
 def inverse_kernel(last, table, partial, out, held, store):
     slots = partial.shape[0]
+    ready = slots - last.shape[2]
 
     def store_slot(s):
-        return pltpu.make_async_copy(held.at[s], out.at[s], store.at[s])
-
-    for s in range(slots):
-        block = last[:, s].reshape(table.shape[1], last.shape[-1])
+        source = partial.at[s] if s < ready else held.at[s - ready]
+        return pltpu.make_async_copy(source, out.at[s], store.at[s])
+
+    for s in range(ready):
+        store_slot(s).start()
+    for s in range(ready, slots):
+        block = last[:, :, s - ready].reshape(table.shape[1], last.shape[-1])
         total = jnp.dot(table[...], block, preferred_element_type=F32)
-        held[s] = (partial[s].astype(F32) + total).astype(BF16)
+        held[s - ready] = (partial[s].astype(F32) + total).astype(BF16)
         store_slot(s).start()
     for s in range(slots):
         store_slot(s).wait()
@@ -377,11 +436,14 @@
     packet = (blocks, n, slots, 2 * BLOCK, channels)
     copies = pltpu.SemaphoreType.DMA
     lines = n * 2 * BLOCK
+    tail = min(TAIL, slots)
+    late = max(blocks - HELD, 1)
+    returns = len(homeward_pieces(blocks, slots, slots - tail, blocks - late))
     last, back_table, partial = pl.pallas_call(
         functools.partial(spectral_kernel, "lat", n, live_total * longitudes, share),
         out_shape=(
-            pltpu.VMEM(packet[1:], BF16),
-            pltpu.VMEM((longitudes, lines), BF16),
+            pltpu.VMEM((late, n, tail) + packet[3:], BF16),
+            pltpu.VMEM((longitudes, late * lines), BF16),
             pltpu.VMEM((slots, longitudes, channels), BF16),
         ),
         in_specs=[anywhere] * 9,
@@ -392,11 +454,12 @@
             pltpu.SMEM(row_sum.shape, F32),
             pltpu.VMEM((1, live_total), F32),
             pltpu.VMEM(channel_mix.shape, BF16),
-            pltpu.VMEM((n, 2, channels), F32),
+            pltpu.VMEM((2, 2, channels), F32),
+            pltpu.VMEM((n // 2, 2, channels), F32),
             pltpu.VMEM((n * padded, channels), F32),
             pltpu.VMEM((n * padded, waves), F32),
             pltpu.VMEM((blocks * lines, longitudes), BF16),
-            pltpu.VMEM((longitudes, max(blocks - 1, 1) * lines), BF16),
+            pltpu.VMEM((longitudes, blocks * lines), BF16),
             pltpu.VMEM(packet, BF16),
             pltpu.VMEM(packet, BF16),
             pltpu.VMEM((channels // 128, everything * 2 * BLOCK, 128), F32),
@@ -404,14 +467,14 @@
             pltpu.VMEM((everything, 128), F32),
             pltpu.VMEM(packet, BF16),
             pltpu.VMEM((channels // 128, everything * 2 * BLOCK, 128), F32),
-            pltpu.VMEM((max(blocks - 1, 1),) + packet[1:], BF16),
+            pltpu.VMEM(packet, BF16),
             pltpu.VMEM(base.shape, BF16),
             pltpu.VMEM(legendre.shape, BF16),
             pltpu.VMEM(spectral_gain.shape, F32),
             copies((slots,)), copies((8,)),
-            copies((n,)), copies((n,)),
+            copies((n // 2,)), copies((n // 2,)),
             copies((blocks, n)), copies((blocks, n)), copies((blocks,)),
-            copies((blocks, n)), copies((blocks, n)), copies((blocks,)),
+            copies((returns, n)), copies((returns, n)), copies((returns,)),
         ],
         compiler_params=pltpu.CompilerParams(
             collective_id=0, has_side_effects=True, vmem_limit_bytes=limit
@@ -429,7 +492,7 @@
         in_specs=[vmem, vmem, vmem],
         out_specs=anywhere,
         scratch_shapes=[
-            pltpu.VMEM((slots, longitudes, channels), BF16),
+            pltpu.VMEM((tail, longitudes, channels), BF16),
             copies((slots,)),
         ],
         compiler_params=pltpu.CompilerParams(vmem_limit_bytes=16 * 1024 * 1024),

time: 130 us -> 129 us (level)
  no operation moved by 1% of the time
where the time goes in v5:
time: 129 us
  Pallas kernels  129 us (100%)
    pallas_call x1, Pallas kernels, body(): pl.pallas_call(functools.partial(spectral_kernel, 'lat', n, live_total *...  126 us

profile of v5, /device:TPU:13, one launch (start us, length us, event | category | flops | bytes accessed | tf_op | source)
XLA Modules:
  0.0 128.9 jit_solution(18145775937188822583)
XLA Ops:
  0.0 126.4 %shard_map.91 = (bf16[2,16,3,16,256]{4,3,2,1,0:T(8,128)(2,1)S(1)}, bf16[1440,512]{1,0:T(8,128)(2,1)S(1)}, bf16[7,1440,256]{2,1,0:T(8,128)(2,1)S(1)}) custom-call(s32[16]{0:T(128)} %counts_far.1, s32[384]{0:T(512)} %owner_far.1, f32[768]{0:T(1024)} %constant.5.clone.row_sum_far, bf16[7,1440,256]{2,1,0:T(8,128)(2,1)} %x.1, ...), custom_call_target="tpu_custom_call" | custom-call | tf_op jit(solution)/shard_map/pallas_call | solution.py:442
  126.4 2.5 %shard_map.92 = bf16[7,1440,256]{2,1,0:T(8,128)(2,1)} custom-call(bf16[2,16,3,16,256]{4,3,2,1,0:T(8,128)(2,1)S(1)} %get-tuple-element.8.last, bf16[1440,512]{1,0:T(8,128)(2,1)S(1)} %get-tuple-element.9.table, bf16[7,1440,256]{2,1,0:T(8,128)(2,1)S(1)} %get-tuple-element.10.partial), custom_call_target="tpu_custom_call" | custom-call | tf_op jit(solution)/shard_map/pallas_call | solution.py:489

commit v6 on v5

--- a/solution.py
+++ b/solution.py
@@ -208,26 +208,32 @@
     counts_copy.wait()
     live = counts[me]
     nothing = jnp.zeros((group, channels), F32)
-    first, second = lax.fori_loop(
-        0, slots, functools.partial(add_slot, live), (nothing, nothing)
-    )
-    halves_of[0, 0:1, :] = jnp.sum(first, axis=0, keepdims=True)
-    halves_of[0, 1:2, :] = jnp.sum(second, axis=0, keepdims=True)
-    partner_copy().start()
-    partner_copy().wait()
-    sums[pair] = halves_of[0] + halves_of[1]
-    lax.fori_loop(1, pairs, start_moment, 0)
+
+    def share_moments(first, second):
+        halves_of[0, 0:1, :] = jnp.sum(first, axis=0, keepdims=True)
+        halves_of[0, 1:2, :] = jnp.sum(second, axis=0, keepdims=True)
+        partner_copy().start()
+        partner_copy().wait()
+        sums[pair] = halves_of[0] + halves_of[1]
+        lax.fori_loop(1, pairs, start_moment, 0)
+
+    if blocks == 1:
+        share_moments(*lax.fori_loop(
+            0, slots, functools.partial(add_slot, live), (nothing, nothing)
+        ))
     for b in range(1, blocks):
         choose_rows(b)
         build_table(b)
 
         def slot_step(s, carry):
             transform(b, s)
-            return carry
-
-        lax.fori_loop(0, slots, slot_step, 0)
+            return add_slot(live, s, carry) if b == 1 else carry
+
+        totals = lax.fori_loop(0, slots, slot_step, (nothing, nothing))
         send_slices(b, 0, slots)
         own_copy(b).start()
+        if b == 1:
+            share_moments(*totals)
 
     split = held_back * lines
     for b in range(blocks):

time: 129 us -> 129 us (level)
  no operation moved by 1% of the time
where the time goes in v6:
time: 129 us; the launch traced here: 128 us
  Pallas kernels  128 us (99%)
    pallas_call x1, Pallas kernels, body(): pl.pallas_call(functools.partial(spectral_kernel, 'lat', n, live_total *...  126 us

profile of v6, /device:TPU:13, one launch (start us, length us, event | category | flops | bytes accessed | tf_op | source)
XLA Modules:
  0.0 128.4 jit_solution(14005643539795413542)
XLA Ops:
  0.0 125.9 %shard_map.91 = (bf16[2,16,3,16,256]{4,3,2,1,0:T(8,128)(2,1)S(1)}, bf16[1440,512]{1,0:T(8,128)(2,1)S(1)}, bf16[7,1440,256]{2,1,0:T(8,128)(2,1)S(1)}) custom-call(s32[16]{0:T(128)} %counts_far.1, s32[384]{0:T(512)} %owner_far.1, f32[768]{0:T(1024)} %constant.5.clone.row_sum_far, bf16[7,1440,256]{2,1,0:T(8,128)(2,1)} %x.1, ...), custom_call_target="tpu_custom_call" | custom-call | tf_op jit(solution)/shard_map/pallas_call | solution.py:448
  125.9 2.5 %shard_map.92 = bf16[7,1440,256]{2,1,0:T(8,128)(2,1)} custom-call(bf16[2,16,3,16,256]{4,3,2,1,0:T(8,128)(2,1)S(1)} %get-tuple-element.8.last, bf16[1440,512]{1,0:T(8,128)(2,1)S(1)} %get-tuple-element.9.table, bf16[7,1440,256]{2,1,0:T(8,128)(2,1)S(1)} %get-tuple-element.10.partial), custom_call_target="tpu_custom_call" | custom-call | tf_op jit(solution)/shard_map/pallas_call | solution.py:495
